TPU v7x, 256 devices: a whole 4x4x8 slice. The times are simulated.
256 devices in a mesh: outer: 8 (over x, y_hi), inner: 32 (over y_lo, z, core).
Axes of the slice: x: 4, y: 4 (y_hi: 2, y_lo: 2; y = y_hi * 2 + y_lo), z: 8, core: 2. Of those that a mesh axis runs over, the one named last changes fastest.
Arguments:
- tokens: bfloat16 [32768, 4096], P('inner', 'outer'), may hold values from -6 to 6
- cotangent: bfloat16 [32768, 4096], P('inner', 'outer'), may hold values from -0.03125 to 0.03125
- weight_cache: bfloat16 [4096, 4096], P(None, 'outer'), may hold values from -0.09375 to 0.09375
- weight_delta: bfloat16 [4096, 4096], P('inner', 'outer'), may hold values from -0.078125 to 0.078125
- sign_bits: int32 [4096], P('outer'), may hold values from 0 to 1
- master: float32 [4096, 4096], P('inner', 'outer'), may hold values from -1.5 to 1.5
- moment: float32 [4096, 4096], P('inner', 'outer'), may hold values from -6 to 6
- variance: float32 [4096, 4096], P('inner', 'outer'), may hold values from 0.25 to 4
Outputs:
- activation: float32 [32768, 4096], P('inner', 'outer')
- new_master: float32 [4096, 4096], P('inner', 'outer')
- new_moment: float32 [4096, 4096], P('inner', 'outer')
- new_variance: float32 [4096, 4096], P('inner', 'outer')
- block_scales: float32 [4096, 32], P('inner', 'outer')
All inputs are finite; a program needn't handle non-finite values.
Results may differ from a plain program's by a relative error of at most 0.003.
Values may be sent and summed in bfloat16 or wider, within the bound.
A program may use at most 128 MiB of HBM per device.

v0:
```python
import jax
import jax.numpy as jnp
from jax import lax
from jax.sharding import Mesh
from jax.sharding import PartitionSpec as P

BLOCK = 128
INNER = ("inner_0", "inner_1", "inner_2")


def split_up(value, dim, devices):
    before, after = (value.shape[:dim], value.shape[dim + 1 :])
    return jnp.moveaxis(value.reshape(*before, devices, -1, *after), dim, 0)


def summed_rows(value, chips, core, dim):
    sizes = (lax.axis_size(chips), lax.axis_size(core))
    blocks = split_up(value, dim, sizes[0] * sizes[1])
    inside = blocks.shape[1:]
    blocks = blocks.reshape(*sizes, *inside).swapaxes(0, 1).reshape(-1, *inside)
    blocks = lax.psum_scatter(blocks, core, scatter_dimension=0, tiled=True)
    return lax.psum_scatter(blocks, chips, scatter_dimension=0, tiled=True)[0]


def hadamard_table(length):
    first = jnp.arange(length, dtype=jnp.int32)[:, None]
    second = jnp.arange(length, dtype=jnp.int32)[None, :]
    common = jnp.bitwise_and(first, second)
    parity = jnp.zeros((length, length), jnp.int32)
    for place in range(length.bit_length() - 1):
        parity = parity + jnp.bitwise_and(jnp.right_shift(common, place), 1)
    return (1 - 2 * (parity % 2)).astype(jnp.float32) / jnp.sqrt(jnp.float32(length))


def smooth(values, signs, table):
    height = values.shape[0]
    blocks = values.reshape(height, -1, table.shape[0]) * signs.reshape(-1, table.shape[0])
    mixed = jnp.einsum("rbk,kj->rbj", blocks, table, precision=lax.Precision.HIGHEST)
    return mixed.reshape(height, -1)


def unsmooth(values, signs, table):
    height = values.shape[0]
    blocks = values.reshape(height, -1, table.shape[0])
    mixed = jnp.einsum("rbj,jk->rbk", blocks, table, precision=lax.Precision.HIGHEST)
    return (mixed * signs.reshape(-1, table.shape[0])).reshape(height, -1)


def outer_product(left, right):
    return lax.dot_general(
        left, right, (((0,), (0,)), ((), ())), preferred_element_type=jnp.float32
    )


def body(tokens, cotangent, weight_cache, weight_delta, sign_bits, master, moment, variance):
    table = hadamard_table(BLOCK)
    signs = (1 - 2 * sign_bits).astype(jnp.float32)
    shard_rows = master.shape[0]
    gathered = lax.all_gather(tokens, "outer", axis=1, tiled=True)
    merged = (
        weight_cache.astype(jnp.float32)
        + lax.all_gather(weight_delta, INNER, axis=0, tiled=True).astype(jnp.float32)
    ).astype(jnp.bfloat16)
    columns = gathered
    output = jnp.dot(columns, merged, preferred_element_type=jnp.float32)
    columns = gathered
    partial_value = outer_product(columns, cotangent)
    summed = summed_rows(partial_value, ("inner_0", "inner_1"), "inner_2", 0)
    smoothed = smooth(summed, signs, table)
    block_scales = jnp.max(jnp.abs(smoothed.reshape(shard_rows, -1, BLOCK)), axis=2)
    restored = unsmooth(smoothed, signs, table)
    new_moment = 0.9 * moment + 0.1 * restored
    new_variance = 0.95 * variance + 0.05 * restored * restored
    corrected = new_moment / (1.0 - 0.9**10)
    spread = jnp.sqrt(new_variance / (1.0 - 0.95**10)) + 1e-08
    new_master = master - 0.01 * (corrected / spread + 0.1 * master)
    return (output, new_master, new_moment, new_variance, block_scales)


def solution(mesh):
    torus = Mesh(
        mesh.devices.reshape(mesh.shape["outer"], 2, 8, 2),
        ("outer", "inner_0", "inner_1", "inner_2"),
    )
    in_specs = (
        P(INNER, "outer"),
        P(INNER, "outer"),
        P(None, "outer"),
        P(INNER, "outer"),
        P("outer"),
        P(INNER, "outer"),
        P(INNER, "outer"),
        P(INNER, "outer"),
    )
    out_specs = (
        P(INNER, "outer"),
        P(INNER, "outer"),
        P(INNER, "outer"),
        P(INNER, "outer"),
        P(INNER, "outer"),
    )
    return jax.shard_map(body, mesh=torus, in_specs=in_specs, out_specs=out_specs, check_vma=False)
```

profile of v0, /device:TPU:6, one launch (start us, length us, event | category | flops | bytes accessed | tf_op | source)
XLA Modules:
  0.0 268.3 jit_solution(17581240308026730228)
XLA Ops:
  8.0 0.0 copy-start
  8.0 0.0 all-gather.5.cloned.1.call-start
  8.1 0.7 all-gather.5.cloned.1.call-update
  8.7 0.0 reduce-scatter.3.cloned.1.call-start
  8.8 129.7 %all-gather.5.cloned.1.call-done = bf16[1024,4096]{1,0:T(8,128)(2,1)} async-done(((bf16[1024,512]{1,0:T(8,128)(2,1)}), bf16[1024,4096]{1,0:T(8,128)(2,1)}) %all-gather.5.cloned.1.call-update) | async-done | bytes 8388624 | tf_op jit(solution)/shard_map/all_gather | solution.py:59
  138.5 0.0 copy-done
  138.5 7.1 %fusion.47 = f32[4096,512]{1,0:T(8,128)S(1)} fusion(bf16[1024,4096]{1,0:T(8,128)(2,1)} %all-gather.5.cloned.1.call-done, bf16[1024,512]{1,0:T(8,128)(2,1)S(1)} %copy-done), kind=kOutput, calls=%fused_computation.54 | convolution fusion | flops 4294967296 | bytes 17825792 | tf_op jit(solution)/shard_map/dot_general | solution.py:50
  145.6 4.2 %copy.19 = f32[16,2,128,512]{3,2,0,1:T(8,128)} copy(f32[16,2,128,512]{3,2,1,0:T(8,128)S(1)} %bitcast.21) | data formatting | bytes 16777216 | tf_op jit(solution)/shard_map/reshape;reshape | solution.py:20
  149.9 0.0 copy-start.2
  149.9 0.0 reduce-scatter.3.cloned.1.call-update
  149.9 0.0 all-gather.3.cloned.1.call-start
  150.0 0.5 all-gather.3.cloned.1.call-update
  150.5 0.0 reduce-scatter.5.cloned.1.call-start
  150.6 20.5 %reduce-scatter.3.cloned.1.call-done = f32[16,128,512]{2,1,0:T(8,128)} async-done(((f32[32,128,512]{2,1,0:T(8,128)}), f32[16,128,512]{2,1,0:T(8,128)}) %reduce-scatter.3.cloned.1.call-update) | async-done | bytes 4194320 | tf_op jit(solution)/shard_map/reduce_scatter | solution.py:21
  171.0 0.0 reduce-scatter.5.cloned.1.call-update
  171.1 0.0 copy-done.2
  171.1 0.0 copy-start.1
  171.1 57.4 %all-gather.3.cloned.1.call-done = bf16[4096,512]{1,0:T(8,128)(2,1)} async-done(((bf16[128,512]{1,0:T(8,128)(2,1)}), bf16[4096,512]{1,0:T(8,128)(2,1)}) %all-gather.3.cloned.1.call-update) | async-done | bytes 4194320 | tf_op jit(solution)/shard_map/all_gather | solution.py:62
  228.5 9.6 %fusion.1 = f32[1024,512]{0,1:T(8,128)S(1)} fusion(bf16[1024,4096]{1,0:T(8,128)(2,1)} %all-gather.5.cloned.1.call-done, bf16[4096,512]{1,0:T(8,128)(2,1)} %all-gather.3.cloned.1.call-done, bf16[4096,512]{1,0:T(8,128)(2,1)} %param.10), kind=kOutput, calls=%fused_computation.2 | convolution fusion | flops 4303355904 | bytes 18874368 | tf_op jit(solution)/shard_map/dot_general | solution.py:65
  238.0 1.8 copy.26
  239.9 16.5 %reduce-scatter.5.cloned.1.call-done = f32[1,128,512]{2,1,0:T(8,128)} async-done(((f32[16,128,512]{2,1,0:T(8,128)}), f32[1,128,512]{2,1,0:T(8,128)}) %reduce-scatter.5.cloned.1.call-update) | async-done | bytes 262160 | tf_op jit(solution)/shard_map/reduce_scatter | solution.py:22
  256.4 1.1 copy.20
  257.5 1.1 abs_reduce_fusion
  258.6 0.4 convolution_multiply_fusion
  259.0 0.1 copy.23
  259.2 0.0 copy-done.1
  259.2 2.0 multiply_subtract_fusion
  (1 shorter events, 0.0 us)
Async XLA Ops:
  8.0 130.5 %copy-start = (bf16[1024,512]{1,0:T(8,128)(2,1)S(1)}, bf16[1024,512]{1,0:T(8,128)(2,1)}, u32[]{:S(2)}) copy-start(bf16[1024,512]{1,0:T(8,128)(2,1)} %param.9) | copy-start | bytes 3145732
  8.0 130.5 %all-gather.5.cloned.1.call-start = ((), (), s32[]{:S(2)}) async-start(), calls=%async_computation.3 | async-start | bytes 9437184 | tf_op jit(solution)/shard_map/all_gather | solution.py:59
  8.7 162.3 %reduce-scatter.3.cloned.1.call-start = ((), (), s32[]{:S(2)}) async-start(), calls=%async_computation.4 | async-start | bytes 12582912 | tf_op jit(solution)/shard_map/reduce_scatter | solution.py:21
  149.9 21.2 %copy-start.2 = (s32[512]{0:T(512)S(1)}, s32[512]{0:T(512)}, u32[]{:S(2)}) copy-start(s32[512]{0:T(512)} %param.12) | copy-start | bytes 6148
  149.9 78.5 %all-gather.3.cloned.1.call-start = ((), (), s32[]{:S(2)}) async-start(), calls=%async_computation.2 | async-start | bytes 4325376 | tf_op jit(solution)/shard_map/all_gather | solution.py:62
  150.5 105.9 %reduce-scatter.5.cloned.1.call-start = ((), (), s32[]{:S(2)}) async-start(), calls=%async_computation.5 | async-start | bytes 4456448 | tf_op jit(solution)/shard_map/reduce_scatter | solution.py:22
  171.1 88.1 %copy-start.1 = (f32[128,512]{1,0:T(8,128)S(1)}, f32[128,512]{1,0:T(8,128)}, u32[]{:S(2)}) copy-start(f32[128,512]{1,0:T(8,128)} %param.13) | copy-start | bytes 786436
Sparse Core Ops, SparseCore 0:
  11.3 127.1 all-gather.4
  150.0 20.9 reduce-scatter.2
  173.6 82.7 reduce-scatter.4
Sparse Core Ops, SparseCore 1:
  152.3 76.1 all-gather.2
where the time goes:
time: 268 us
  waiting for transfers between devices  225 us (84%)
  matrix products  18.3 us (7%)
  between operations  15.3 us (6%)
  local copies, waits for them, and re-layouts  7.28 us (3%)
    all_gather x1, waiting for transfers between devices, body(): gathered = lax.all_gather(tokens, 'outer', axis=1, tiled=True)  130 us
    all_gather x1, waiting for transfers between devices, body(): lax.all_gather(weight_delta, INNER, axis=0, tiled=True).astype(jnp.float32)  57.4 us
    reduce_scatter x1, waiting for transfers between devices, summed_rows(): blocks = lax.psum_scatter(blocks, core, scatter_dimension=0, tiled=True)  20.5 us
    reduce_scatter x1, waiting for transfers between devices, summed_rows(): return lax.psum_scatter(blocks, chips, scatter_dimension=0, tiled=True)[0]  16.5 us
    dot_general x1, matrix products, body(): output = jnp.dot(columns, merged, preferred_element_type=jnp.float32)  9.58 us
    dot_general x1, matrix products, outer_product(): lax.dot_general(left, right, (((0,), (0,)), ((), ())), preferred_element_...  7.13 us
  transfers between devices with their start and end apart: 4, of which 4 were waited for; matrix products, arithmetic and copies ran while one was open for 4% of the time, Pallas kernels for 0%

commit v1 on v0

--- a/solution.py
+++ b/solution.py
@@ -6,6 +6,9 @@
 
 BLOCK = 128
 INNER = ("inner_0", "inner_1", "inner_2")
+quotas_rest = lambda s0: jnp.concatenate(
+    lax.all_to_all(jnp.stack(lax.psum(1, INNER) * [s0]), INNER, 0, 0), axis=0
+)
 
 
 def split_up(value, dim, devices):
@@ -58,8 +61,7 @@
     shard_rows = master.shape[0]
     gathered = lax.all_gather(tokens, "outer", axis=1, tiled=True)
     merged = (
-        weight_cache.astype(jnp.float32)
-        + lax.all_gather(weight_delta, INNER, axis=0, tiled=True).astype(jnp.float32)
+        weight_cache.astype(jnp.float32) + quotas_rest(weight_delta).astype(jnp.float32)
     ).astype(jnp.bfloat16)
     columns = gathered
     output = jnp.dot(columns, merged, preferred_element_type=jnp.float32)

time: 268 us -> 316 us (1.18)
  waiting for transfers between devices: 225 us -> 263 us
  starting transfers between devices: 0.16 us -> 7.67 us
  local copies, waits for them, and re-layouts: 7.28 us -> 10.6 us
    all_to_all x0 -> x1, waiting for transfers between devices: none -> 114 us  [lax.all_to_all(jnp.stack(lax.psum(1, INNER) * [s0]), INNER, 0, 0)]
    all_gather x1 -> x0, waiting for transfers between devices: 57.4 us -> none  [body(): lax.all_gather(weight_delta, INNER, axis=0, tiled=True).astype(jnp.float32)]
    reduce_scatter x1, waiting for transfers between devices: 20.5 us -> 10.2 us  [summed_rows(): blocks = lax.psum_scatter(blocks, core, scatter_dimension=0, tiled=True)]
    reduce_scatter x1, waiting for transfers between devices: 16.5 us -> 8.3 us  [summed_rows(): return lax.psum_scatter(blocks, chips, scatter_dimension=0, tiled=True)[0]]
    all_to_all x0 -> x1, starting transfers between devices: none -> 7.55 us  [lax.all_to_all(jnp.stack(lax.psum(1, INNER) * [s0]), INNER, 0, 0)]
where the time goes in v1:
time: 316 us
  waiting for transfers between devices  263 us (83%)
  matrix products  18.2 us (6%)
  between operations  13.8 us (4%)
  local copies, waits for them, and re-layouts  10.6 us (3%)
  starting transfers between devices  7.67 us (2%)
    all_gather x1, waiting for transfers between devices, body(): gathered = lax.all_gather(tokens, 'outer', axis=1, tiled=True)  130 us
    all_to_all x1, waiting for transfers between devices, lax.all_to_all(jnp.stack(lax.psum(1, INNER) * [s0]), INNER, 0, 0)  114 us
    reduce_scatter x1, waiting for transfers between devices, summed_rows(): blocks = lax.psum_scatter(blocks, core, scatter_dimension=0, tiled=True)  10.2 us
    dot_general x1, matrix products, body(): output = jnp.dot(columns, merged, preferred_element_type=jnp.float32)  9.57 us
    reduce_scatter x1, waiting for transfers between devices, summed_rows(): return lax.psum_scatter(blocks, chips, scatter_dimension=0, tiled=True)[0]  8.3 us
    all_to_all x1, starting transfers between devices, lax.all_to_all(jnp.stack(lax.psum(1, INNER) * [s0]), INNER, 0, 0)  7.55 us
    dot_general x1, matrix products, outer_product(): lax.dot_general(left, right, (((0,), (0,)), ((), ())), preferred_element_...  7.13 us
  transfers between devices with their start and end apart: 4, of which 4 were waited for; matrix products, arithmetic and copies ran while one was open for 4% of the time, Pallas kernels for 0%

profile of v1, /device:TPU:6, one launch (start us, length us, event | category | flops | bytes accessed | tf_op | source)
XLA Modules:
  0.0 315.6 jit_solution(1942898206413471297)
XLA Ops:
  7.2 0.0 copy-start
  7.2 0.0 all-gather.2.cloned.1.call-start
  7.2 0.7 all-gather.2.cloned.1.call-update
  7.9 0.0 reduce-scatter.3.cloned.1.call-start
  8.0 129.7 %all-gather.2.cloned.1.call-done = bf16[1024,4096]{1,0:T(8,128)(2,1)} async-done(((bf16[1024,512]{1,0:T(8,128)(2,1)}), bf16[1024,4096]{1,0:T(8,128)(2,1)}) %all-gather.2.cloned.1.call-update) | async-done | bytes 8388624 | tf_op jit(solution)/shard_map/all_gather | solution.py:62
  137.7 0.0 copy-done
  137.7 7.1 %fusion.51 = f32[4096,512]{1,0:T(8,128)S(1)} fusion(bf16[1024,4096]{1,0:T(8,128)(2,1)} %all-gather.2.cloned.1.call-done, bf16[1024,512]{1,0:T(8,128)(2,1)S(1)} %copy-done), kind=kOutput, calls=%fused_computation.55 | convolution fusion | flops 4294967296 | bytes 17825792 | tf_op jit(solution)/shard_map/dot_general | solution.py:53
  144.8 4.2 %copy.19 = f32[16,2,128,512]{3,2,0,1:T(8,128)} copy(f32[16,2,128,512]{3,2,1,0:T(8,128)S(1)} %bitcast.23) | data formatting | bytes 16777216 | tf_op jit(solution)/shard_map/reshape;reshape | solution.py:23
  149.1 0.0 copy-start.2
  149.1 0.0 reduce-scatter.3.cloned.1.call-update
  149.1 0.9 copy-done.2
  150.0 0.0 copy-start.3
  150.0 2.4 stack.2
  152.4 7.6 %all-to-all-start = ((bf16[32,128,512]{2,1,0:T(8,128)(2,1)}), bf16[32,128,512]{2,1,0:T(8,128)(2,1)}, u32[]{:S(2)}, u32[]{:S(2)}) async-start(bf16[32,128,512]{2,1,0:T(8,128)(2,1)} %stack.2), calls=%async_computation | async-start | bytes 8388608 | tf_op jit(solution)/shard_map/all_to_all | solution.py:10
  160.0 0.0 reduce-scatter.5.cloned.1.call-start
  160.0 10.2 %reduce-scatter.3.cloned.1.call-done = f32[16,128,512]{2,1,0:T(8,128)} async-done(((f32[32,128,512]{2,1,0:T(8,128)}), f32[16,128,512]{2,1,0:T(8,128)}) %reduce-scatter.3.cloned.1.call-update) | async-done | bytes 4194320 | tf_op jit(solution)/shard_map/reduce_scatter | solution.py:24
  170.2 0.0 reduce-scatter.5.cloned.1.call-update
  170.2 0.0 copy-done.3
  170.3 114.3 %all-to-all-done = bf16[32,128,512]{2,1,0:T(8,128)(2,1)} async-done(((bf16[32,128,512]{2,1,0:T(8,128)(2,1)}), bf16[32,128,512]{2,1,0:T(8,128)(2,1)}, u32[]{:S(2)}, u32[]{:S(2)}) %all-to-all-start) | async-done | bytes 4194336 | tf_op jit(solution)/shard_map/all_to_all | solution.py:10
  284.6 0.0 copy-start.1
  284.6 9.6 %fusion.3 = f32[1024,512]{0,1:T(8,128)S(1)} fusion(bf16[1024,4096]{1,0:T(8,128)(2,1)} %all-gather.2.cloned.1.call-done, bf16[4096,512]{1,0:T(8,128)(2,1)} %bitcast.9, bf16[4096,512]{1,0:T(8,128)(2,1)} %param.10), kind=kOutput, calls=%fused_computation.3 | convolution fusion | flops 4303355904 | bytes 18874368 | tf_op jit(solution)/shard_map/dot_general | solution.py:67
  294.2 1.8 copy.26
  296.0 8.3 %reduce-scatter.5.cloned.1.call-done = f32[1,128,512]{2,1,0:T(8,128)} async-done(((f32[16,128,512]{2,1,0:T(8,128)}), f32[1,128,512]{2,1,0:T(8,128)}) %reduce-scatter.5.cloned.1.call-update) | async-done | bytes 262160 | tf_op jit(solution)/shard_map/reduce_scatter | solution.py:25
  304.3 1.1 copy.20
  305.4 1.1 abs_reduce_fusion
  306.5 0.4 convolution_multiply_fusion
  306.9 0.1 copy.23
  307.1 0.0 copy-done.1
  307.1 2.0 multiply_subtract_fusion
  (1 shorter events, 0.0 us)
Async XLA Ops:
  7.2 130.5 %copy-start = (bf16[1024,512]{1,0:T(8,128)(2,1)S(1)}, bf16[1024,512]{1,0:T(8,128)(2,1)}, u32[]{:S(2)}) copy-start(bf16[1024,512]{1,0:T(8,128)(2,1)} %param.9) | copy-start | bytes 3145732
  7.2 130.5 %all-gather.2.cloned.1.call-start = ((), (), s32[]{:S(2)}) async-start(), calls=%async_computation.3 | async-start | bytes 9437184 | tf_op jit(solution)/shard_map/all_gather | solution.py:62
  7.9 162.3 %reduce-scatter.3.cloned.1.call-start = ((), (), s32[]{:S(2)}) async-start(), calls=%async_computation.4 | async-start | bytes 12582912 | tf_op jit(solution)/shard_map/reduce_scatter | solution.py:24
  149.1 0.9 copy-start.2
  150.0 20.3 %copy-start.3 = (s32[512]{0:T(512)S(1)}, s32[512]{0:T(512)}, u32[]{:S(2)}) copy-start(s32[512]{0:T(512)} %param.12) | copy-start | bytes 6148
  152.4 132.2 %all-to-all-start = ((bf16[32,128,512]{2,1,0:T(8,128)(2,1)}), bf16[32,128,512]{2,1,0:T(8,128)(2,1)}, u32[]{:S(2)}, u32[]{:S(2)}) async-start(bf16[32,128,512]{2,1,0:T(8,128)(2,1)} %stack.2), calls=%async_computation | async-start | bytes 8388608 | tf_op jit(solution)/shard_map/all_to_all | solution.py:10
  160.0 144.3 %reduce-scatter.5.cloned.1.call-start = ((), (), s32[]{:S(2)}) async-start(), calls=%async_computation.5 | async-start | bytes 4456448 | tf_op jit(solution)/shard_map/reduce_scatter | solution.py:25
  284.6 22.5 %copy-start.1 = (f32[128,512]{1,0:T(8,128)S(1)}, f32[128,512]{1,0:T(8,128)}, u32[]{:S(2)}) copy-start(f32[128,512]{1,0:T(8,128)} %param.13) | copy-start | bytes 786436
Sparse Core Ops, SparseCore 0:
  10.5 127.1 all-gather.1
  149.2 20.9 reduce-scatter.2
  172.8 131.4 reduce-scatter.4
